TPU v7x, 32 devices: a whole 2x2x4 slice. The times are simulated.
32 devices in a mesh: ta: 8 (over y, x, core), ga: 4 (over z).
Axes of the slice: x: 2, y: 2, z: 4, core: 2. Of those that a mesh axis runs over, the one named last changes fastest.
Arguments:
- snapshots: bfloat16 [1024, 4, 16384], P('ta', 'ga'), may hold values from -12 to 12
- block_starts: int32 [7], replicated, may hold values from 0 to 768
- kept_freqs: int32 [32], replicated, may hold values from 0 to 128
Outputs:
- spectra: bfloat16 [4, 7, 2, 32, 16384], P('ga', None, None, None, 'ta')
- power_step: float32 [4, 7, 2, 32, 16384], P('ga', None, None, None, 'ta')
All inputs are finite; a program needn't handle non-finite values.
Results may differ from a plain program's by a relative error of at most 0.0047.
Values may be sent and summed in bfloat16 or wider, within the bound.
A program may use at most 192 MiB of HBM per device.

v0:
```python
import math
import jax
import jax.numpy as jnp
from jax import lax
from jax.sharding import PartitionSpec as P

NFFT = 256
NB = 7
NF = 32


def kernel_table(kept_freqs, sample_index):
    phase_index = kept_freqs[:, None] * sample_index[None, :] % NFFT
    angle_val = 2.0 * math.pi / NFFT * phase_index.astype(jnp.float32)
    window = 0.5 - 0.5 * jnp.cos(2.0 * math.pi / NFFT * sample_index.astype(jnp.float32))
    norm_scale = 2.0 / math.sqrt(NFFT)
    real_rows = window[None, :] * jnp.cos(angle_val) * norm_scale
    imag_rows = -window[None, :] * jnp.sin(angle_val) * norm_scale
    return jnp.concatenate([real_rows, imag_rows], axis=0)


def transform(series, kernel_rows, block_starts):
    blocks = []
    for block_index in range(NB):
        segment = lax.dynamic_slice_in_dim(series, block_starts[block_index], NFFT, 0)
        blocks.append(jnp.dot(kernel_rows, segment, preferred_element_type=jnp.float32))
    return jnp.stack(blocks).astype(jnp.bfloat16)


def gram_terms(spectra):
    values = spectra.reshape(NB, 2, NF, -1)
    real_part = values[:, 0]
    imag_part = values[:, 1]
    f32 = jnp.float32
    gram_re = jnp.einsum(
        "bfp,cfp->fbc", real_part, real_part, preferred_element_type=f32
    ) + jnp.einsum("bfp,cfp->fbc", imag_part, imag_part, preferred_element_type=f32)
    gram_im = jnp.einsum(
        "bfp,cfp->fbc", real_part, imag_part, preferred_element_type=f32
    ) - jnp.einsum("bfp,cfp->fbc", imag_part, real_part, preferred_element_type=f32)
    return (gram_re, gram_im)


def power_apply(spectra, gram_re, gram_im):
    values = spectra.astype(jnp.float32).reshape(NB, 2, NF, -1)
    real_part = values[:, 0]
    imag_part = values[:, 1]
    highest = lax.Precision.HIGHEST
    out_re = jnp.einsum("cfp,fcb->bfp", real_part, gram_re, precision=highest) - jnp.einsum(
        "cfp,fcb->bfp", imag_part, gram_im, precision=highest
    )
    out_im = jnp.einsum("cfp,fcb->bfp", real_part, gram_im, precision=highest) + jnp.einsum(
        "cfp,fcb->bfp", imag_part, gram_re, precision=highest
    )
    return jnp.stack([out_re, out_im], axis=1)


def shards(snapshots, block_starts, kept_freqs):
    ta_count = lax.axis_size("ta")
    ga_count = lax.axis_size("ga")
    local_times = snapshots.shape[0]
    own_pts = snapshots.shape[2] // ta_count
    kernel_rows = kernel_table(kept_freqs, jnp.arange(NFFT, dtype=jnp.int32)).astype(jnp.bfloat16)
    shaped = snapshots.reshape(local_times, ta_count, own_pts)
    arrived = lax.all_to_all(shaped, "ta", split_axis=1, concat_axis=0, tiled=True)
    spectra = transform(
        arrived.reshape(arrived.shape[0], arrived.shape[2]), kernel_rows, block_starts
    )
    late_sums = gram_terms(spectra)
    summed = lax.psum((late_sums[0], late_sums[1]), ("ta", "ga"))
    denominator = float(NB * own_pts * ta_count * ga_count)
    gram_re = summed[0] / denominator
    gram_im = summed[1] / denominator
    power = power_apply(spectra, gram_re, gram_im)
    return (spectra.reshape(1, NB, 2, NF, own_pts), power.reshape(1, NB, 2, NF, own_pts))


def solution(mesh):
    in_specs = (P("ta", "ga", None), P(), P())
    out_specs = (P("ga", None, None, None, "ta"), P("ga", None, None, None, "ta"))
    return jax.shard_map(shards, mesh=mesh, in_specs=in_specs, out_specs=out_specs, check_vma=False)
```

profile of v0, /device:TPU:0, one launch (start us, length us, event | category | flops | bytes accessed | tf_op | source)
XLA Modules:
  0.0 161.5 jit_solution(14835817679543147446)
XLA Ops:
  0.6 6.4 %copy.43 = bf16[128,1,16384]{0,2,1:T(8,128)(2,1)} copy(bf16[128,1,16384]{2,0,1:T(8,128)(2,1)} %param.3) | data formatting | bytes 8388608 | tf_op args[0]
  7.1 5.3 %all-to-all-start = ((bf16[128,8,2048]{0,2,1:T(8,128)(2,1)}), bf16[128,8,2048]{0,2,1:T(8,128)(2,1)}, u32[]{:S(2)}, u32[]{:S(2)}) async-start(bf16[128,8,2048]{0,2,1:T(8,128)(2,1)} %bitcast.61), calls=%async_computation | async-start | bytes 8388608 | tf_op jit(solution)/shard_map/all_to_all | solution.py:65
  12.4 0.0 copy-done.6
  12.4 0.7 fusion.29
  26.2 0.0 copy-done.7
  26.2 0.2 multiply_convert_fusion.1
  26.4 35.2 %all-to-all-done = bf16[128,8,2048]{0,2,1:T(8,128)(2,1)} async-done(((bf16[128,8,2048]{0,2,1:T(8,128)(2,1)}), bf16[128,8,2048]{0,2,1:T(8,128)(2,1)}, u32[]{:S(2)}, u32[]{:S(2)}) %all-to-all-start) | async-done | bytes 4194336 | tf_op jit(solution)/shard_map/all_to_all | solution.py:65
  61.6 6.5 %copy.44 = bf16[8,128,1,2048]{3,1,0,2:T(8,128)(2,1)} copy(bf16[8,128,1,2048]{1,3,0,2:T(8,128)(2,1)} %bitcast.2) | data formatting | bytes 8388608 | tf_op jit(solution)/shard_map/all_to_all | solution.py:65
  68.1 1.8 %convolution_convert_fusion = bf16[64,2048]{1,0:T(8,128)(2,1)S(1)} fusion(bf16[1024,2048]{1,0:T(8,128)(2,1)} %bitcast.54, s32[]{:T(128)S(6)} %select_n.35, bf16[32,256]{1,0:T(8,128)(2,1)S(1)} %get-tuple-element.20, bf16[32,256]{1,0:T(8,128)(2,1)S(1)} %get-tuple-element.19), kind=kOutput, calls=%fused_computation.5 | convolution fusion | flops 67305472 | bytes 1343492 | tf_op jit(solution)/shard_map/dot_general | solution.py:26
  69.9 1.7 %convolution_convert_fusion.1 = bf16[64,2048]{1,0:T(8,128)(2,1)S(1)} fusion(bf16[1024,2048]{1,0:T(8,128)(2,1)} %bitcast.55, s32[]{:T(128)S(6)} %select_n.34, bf16[32,256]{1,0:T(8,128)(2,1)S(1)} %get-tuple-element.20, bf16[32,256]{1,0:T(8,128)(2,1)S(1)} %get-tuple-element.19), kind=kOutput, calls=%fused_computation.6 | convolution fusion | flops 67305472 | bytes 1343492 | tf_op jit(solution)/shard_map/dot_general | solution.py:26
  71.6 1.7 %convolution_convert_fusion.2 = bf16[64,2048]{1,0:T(8,128)(2,1)S(1)} fusion(bf16[1024,2048]{1,0:T(8,128)(2,1)} %bitcast.56, s32[]{:T(128)S(6)} %select_n.33, bf16[32,256]{1,0:T(8,128)(2,1)S(1)} %get-tuple-element.20, bf16[32,256]{1,0:T(8,128)(2,1)S(1)} %get-tuple-element.19), kind=kOutput, calls=%fused_computation.7 | convolution fusion | flops 67305472 | bytes 1343492 | tf_op jit(solution)/shard_map/dot_general | solution.py:26
  73.2 1.7 %convolution_convert_fusion.3 = bf16[64,2048]{1,0:T(8,128)(2,1)S(1)} fusion(bf16[1024,2048]{1,0:T(8,128)(2,1)} %bitcast.57, s32[]{:T(128)S(6)} %select_n.32, bf16[32,256]{1,0:T(8,128)(2,1)S(1)} %get-tuple-element.20, bf16[32,256]{1,0:T(8,128)(2,1)S(1)} %get-tuple-element.19), kind=kOutput, calls=%fused_computation.8 | convolution fusion | flops 67305472 | bytes 1343492 | tf_op jit(solution)/shard_map/dot_general | solution.py:26
  74.9 0.0 copy-done
  74.9 0.4 convolution_convert_fusion.4
  75.3 0.4 convolution_convert_fusion.5
  75.7 0.4 convolution_convert_fusion.6
  76.2 1.2 copy.46
  77.4 1.2 copy.45
  78.6 1.2 copy.47
  79.8 1.2 copy.48
  81.0 1.2 copy.49
  82.2 1.2 copy.50
  83.4 1.2 copy.51
  84.6 9.9 %stack.64 = bf16[7,2,32,2048]{3,0,2,1:T(8,128)(2,1)S(1)} concatenate(bf16[1,2,32,2048]{3,0,2,1:T(2,128)(2,1)} %copy.45, bf16[1,2,32,2048]{3,0,2,1:T(2,128)(2,1)} %copy.46, bf16[1,2,32,2048]{3,0,2,1:T(2,128)(2,1)} %copy.47, bf16[1,2,32,2048]{3,0,2,1:T(2,128)(2,1)} %copy.48, bf16[1,2,32,2048]{3,0,2,1:T(2,128)(2,1)} %copy.49, bf16[1,2,32,2048]{3,0,2,1:T(2,128)(2,1)} %copy.50, ...), dimensions={0} | concatenate | bytes 3670016 | tf_op jit(solution)/shard_map/stack | solution.py:27
  94.5 1.4 fusion.11
  96.0 1.4 fusion.10
  97.4 1.4 fusion.14
  98.8 0.8 fusion.13
  99.5 1.6 %copy.55 = f32[32,7,7]{0,2,1:T(8,128)} copy(f32[32,7,7]{2,1,0:T(8,128)} %fusion.11) | data formatting | bytes 12544 | tf_op jit(solution)/shard_map/bfp,cfp->fbc/dot_general | solution.py:38
  101.2 1.6 %copy.56 = f32[32,7,7]{0,2,1:T(8,128)} copy(f32[32,7,7]{2,1,0:T(8,128)} %fusion.10) | data formatting | bytes 12544 | tf_op jit(solution)/shard_map/bfp,cfp->fbc/dot_general | solution.py:40
  102.8 1.6 %copy.53 = f32[32,7,7]{0,2,1:T(8,128)} copy(f32[32,7,7]{2,1,0:T(8,128)} %fusion.14) | data formatting | bytes 12544 | tf_op jit(solution)/shard_map/bfp,cfp->fbc/dot_general | solution.py:37
  104.4 0.7 copy.52
  105.1 0.8 sub.22
  105.9 0.8 add.48
  106.7 41.2 %all-reduce = (f32[32,7,7]{0,2,1:T(8,128)S(1)}, f32[32,7,7]{0,2,1:T(8,128)S(1)}) all-reduce(f32[32,7,7]{0,2,1:T(8,128)S(1)} %sub.22, f32[32,7,7]{0,2,1:T(8,128)S(1)} %add.48), channel_id=1, replica_groups=mesh['ta'=8,'ga'=4] {'ta','ga'}, use_global_device_ids=true, to_apply=%region_1.2 | all-reduce | flops 3136 | bytes 25088 | tf_op jit(solution)/shard_map/psum | solution.py:70
  147.9 0.6 broadcast_multiply_fusion
  148.5 0.8 copy.54
  149.3 0.9 copy.57
  150.1 0.0 copy-start.4
  150.2 1.0 constant_dynamic-update-slice_fusion.6
  151.2 1.0 fusion.9
  152.2 1.0 fusion.12
  153.1 1.1 fusion
  154.3 1.1 fusion.1
  155.4 0.7 maximum_bitcast_fusion
  156.2 4.0 %copy.60 = f32[1,7,2,32,2048]{4,3,2,1,0:T(8,128)} copy(f32[1,7,2,32,2048]{4,1,3,2,0:T(8,128)S(1)} %maximum_bitcast_fusion) | data formatting | bytes 7340032
  160.3 0.0 copy-start.5
  160.3 1.2 copy-done.5
  (18 shorter events, 0.2 us)
Async XLA Ops:
  7.1 5.3 %copy-start.6 = (s32[7]{0:T(128)S(1)}, s32[7]{0:T(128)}, u32[]{:S(2)}) copy-start(s32[7]{0:T(128)} %param.4) | copy-start | bytes 88
  7.1 19.1 %copy-start.7 = (s32[32]{0:T(128)S(1)}, s32[32]{0:T(128)}, u32[]{:S(2)}) copy-start(s32[32]{0:T(128)} %param.5) | copy-start | bytes 388
  7.1 54.5 %all-to-all-start = ((bf16[128,8,2048]{0,2,1:T(8,128)(2,1)}), bf16[128,8,2048]{0,2,1:T(8,128)(2,1)}, u32[]{:S(2)}, u32[]{:S(2)}) async-start(bf16[128,8,2048]{0,2,1:T(8,128)(2,1)} %bitcast.61), calls=%async_computation | async-start | bytes 8388608 | tf_op jit(solution)/shard_map/all_to_all | solution.py:65
  68.1 6.8 %copy-start = (bf16[8,128,1,2048]{3,1,0,2:T(8,128)(2,1)S(1)}, bf16[8,128,1,2048]{3,1,0,2:T(8,128)(2,1)}, u32[]{:S(2)}) copy-start(bf16[8,128,1,2048]{3,1,0,2:T(8,128)(2,1)} %copy.44) | copy-start | bytes 12582916
  75.7 5.2 %copy-start.1 = (bf16[64,2048]{1,0:T(8,128)(2,1)}, bf16[64,2048]{1,0:T(8,128)(2,1)S(1)}, u32[]{:S(2)}) copy-start(bf16[64,2048]{1,0:T(8,128)(2,1)S(1)} %convolution_convert_fusion.5) | copy-start | bytes 786436
  76.2 7.2 %copy-start.3 = (bf16[64,2048]{1,0:T(8,128)(2,1)}, bf16[64,2048]{1,0:T(8,128)(2,1)S(1)}, u32[]{:S(2)}) copy-start(bf16[64,2048]{1,0:T(8,128)(2,1)S(1)} %convolution_convert_fusion.6) | copy-start | bytes 786436
  150.1 2.0 %copy-start.4 = (f32[32,7,7]{1,2,0:T(8,128)S(1)}, f32[32,7,7]{1,2,0:T(8,128)}, u32[]{:S(2)}) copy-start(f32[32,7,7]{1,2,0:T(8,128)} %copy.54) | copy-start | bytes 18820
  156.2 4.0 %copy-start.2 = (bf16[64,2048]{1,0:T(8,128)(2,1)S(1)}, bf16[64,2048]{1,0:T(8,128)(2,1)}, u32[]{:S(2)}) copy-start(bf16[64,2048]{1,0:T(8,128)(2,1)} %copy-done.1) | copy-start | bytes 786436
  160.3 1.2 copy-start.5
where the time goes:
time: 163 us; the launch traced here: 162 us
  local copies, waits for them, and re-layouts  45.6 us (28%)
  blocking collectives  41.2 us (25%)
  waiting for transfers between devices  35.2 us (22%)
  matrix products  17.2 us (11%)
  between operations  13.9 us (9%)
  starting transfers between devices  5.33 us (3%)
  other arithmetic  3.17 us (2%)
    psum x1, blocking collectives, shards(): summed = lax.psum((late_sums[0], late_sums[1]), ('ta', 'ga'))  41.2 us
    all_to_all x1, waiting for transfers between devices, shards(): lax.all_to_all(shaped, 'ta', split_axis=1, concat_axis=0, tiled=True)  35.2 us
    another operation x9, local copies, waits for them, and re-layouts, transform(): return jnp.stack(blocks).astype(jnp.bfloat16)  18.4 us
    unnamed x24, local copies, waits for them, and re-layouts  12.7 us
    dot_general x7, matrix products, transform(): jnp.dot(kernel_rows, segment, preferred_element_type=jnp.float32)  8.01 us
    all_to_all x1, local copies, waits for them, and re-layouts, shards(): lax.all_to_all(shaped, 'ta', split_axis=1, concat_axis=0, tiled=True)  6.54 us
    all_to_all x1, starting transfers between devices, shards(): lax.all_to_all(shaped, 'ta', split_axis=1, concat_axis=0, tiled=True)  5.33 us
  transfers between devices with their start and end apart: 1, of which 1 were waited for; matrix products, arithmetic and copies ran while one was open for 1% of the time, Pallas kernels for 0%

commit v1 on v0

--- a/solution.py
+++ b/solution.py
@@ -62,7 +62,10 @@
     own_pts = snapshots.shape[2] // ta_count
     kernel_rows = kernel_table(kept_freqs, jnp.arange(NFFT, dtype=jnp.int32)).astype(jnp.bfloat16)
     shaped = snapshots.reshape(local_times, ta_count, own_pts)
-    arrived = lax.all_to_all(shaped, "ta", split_axis=1, concat_axis=0, tiled=True)
+    arrived = jnp.concatenate(
+        lax.all_to_all(jnp.stack(jnp.split(shaped, lax.axis_size("ta"), axis=1)), "ta", 0, 0),
+        axis=0,
+    )
     spectra = transform(
         arrived.reshape(arrived.shape[0], arrived.shape[2]), kernel_rows, block_starts
     )

time: 163 us -> 177 us (1.086)
  local copies, waits for them, and re-layouts: 45.6 us -> 57 us
    unnamed x24 -> x35, local copies, waits for them, and re-layouts: 12.7 us -> 22.6 us
    dot_general x7, matrix products: 8.01 us -> 5.47 us  [transform(): jnp.dot(kernel_rows, segment, preferred_element_type=jnp.float32)]
where the time goes in v1:
time: 177 us; the launch traced here: 175 us
  local copies, waits for them, and re-layouts  57 us (32%)
  blocking collectives  41.5 us (23%)
  waiting for transfers between devices  35.4 us (20%)
  matrix products  17.9 us (10%)
  between operations  13.7 us (8%)
  starting transfers between devices  5.33 us (3%)
  other arithmetic  4.52 us (3%)
    psum x1, blocking collectives, shards(): summed = lax.psum((late_sums[0], late_sums[1]), ('ta', 'ga'))  41.5 us
    all_to_all x1, waiting for transfers between devices, shards(): lax.all_to_all(jnp.stack(jnp.split(shaped, lax.axis_size('ta'), axis=1)),...  35.4 us
    unnamed x35, local copies, waits for them, and re-layouts  22.6 us
    another operation x9, local copies, waits for them, and re-layouts, transform(): return jnp.stack(blocks).astype(jnp.bfloat16)  18.4 us
    all_to_all x1, local copies, waits for them, and re-layouts, shards(): lax.all_to_all(jnp.stack(jnp.split(shaped, lax.axis_size('ta'), axis=1)),...  6.54 us
    dot_general x7, matrix products, transform(): jnp.dot(kernel_rows, segment, preferred_element_type=jnp.float32)  5.47 us
    all_to_all x1, starting transfers between devices, shards(): lax.all_to_all(jnp.stack(jnp.split(shaped, lax.axis_size('ta'), axis=1)),...  5.33 us
  transfers between devices with their start and end apart: 1, of which 1 were waited for; matrix products, arithmetic and copies ran while one was open for 1% of the time, Pallas kernels for 0%

profile of v1, /device:TPU:0, one launch (start us, length us, event | category | flops | bytes accessed | tf_op | source)
XLA Modules:
  0.0 175.4 jit_solution(6063164927277509246)
XLA Ops:
  0.6 6.4 %copy.67 = bf16[128,1,16384]{0,2,1:T(8,128)(2,1)} copy(bf16[128,1,16384]{2,0,1:T(8,128)(2,1)} %param.3) | data formatting | bytes 8388608 | tf_op args[0]
  7.0 2.0 %fusion.22 = bf16[8,128,1,2048]{1,3,2,0:T(8,128)(2,1)} fusion(bf16[128,8,2048]{0,2,1:T(8,128)(2,1)} %bitcast.90), kind=kLoop, calls=%fused_computation.42 | loop fusion | bytes 1048576
  9.0 1.9 %fusion.21 = bf16[8,128,1,2048]{1,3,2,0:T(8,128)(2,1)} fusion(bf16[8,128,1,2048]{1,3,2,0:T(8,128)(2,1)} %fusion.22, bf16[128,8,2048]{0,2,1:T(8,128)(2,1)} %bitcast.91), kind=kLoop, calls=%fused_computation.40 | loop fusion | bytes 1048576
  10.9 1.9 %fusion.20 = bf16[8,128,1,2048]{1,3,2,0:T(8,128)(2,1)} fusion(bf16[8,128,1,2048]{1,3,2,0:T(8,128)(2,1)} %fusion.21, bf16[128,8,2048]{0,2,1:T(8,128)(2,1)} %bitcast.92), kind=kLoop, calls=%fused_computation.38 | loop fusion | bytes 1048576
  12.8 1.9 %fusion.19 = bf16[8,128,1,2048]{1,3,2,0:T(8,128)(2,1)} fusion(bf16[8,128,1,2048]{1,3,2,0:T(8,128)(2,1)} %fusion.20, bf16[128,8,2048]{0,2,1:T(8,128)(2,1)} %bitcast.93), kind=kLoop, calls=%fused_computation.36 | loop fusion | bytes 1048576
  14.7 0.8 fusion.18
  15.5 0.8 fusion.17
  16.3 0.8 fusion.16
  17.2 0.9 fusion.15
  18.0 5.3 %all-to-all-start = ((bf16[8,128,1,2048]{1,3,2,0:T(8,128)(2,1)}), bf16[8,128,1,2048]{1,3,2,0:T(8,128)(2,1)}, u32[]{:S(2)}, u32[]{:S(2)}) async-start(bf16[8,128,1,2048]{1,3,2,0:T(8,128)(2,1)} %fusion.15), calls=%async_computation | async-start | bytes 8388608 | tf_op jit(solution)/shard_map/all_to_all | solution.py:66
  23.4 0.7 fusion.37
  37.1 35.4 %all-to-all-done = bf16[8,128,1,2048]{1,3,2,0:T(8,128)(2,1)} async-done(((bf16[8,128,1,2048]{1,3,2,0:T(8,128)(2,1)}), bf16[8,128,1,2048]{1,3,2,0:T(8,128)(2,1)}, u32[]{:S(2)}, u32[]{:S(2)}) %all-to-all-start) | async-done | bytes 4194336 | tf_op jit(solution)/shard_map/all_to_all | solution.py:66
  72.5 6.5 %copy.70 = bf16[8,128,1,2048]{3,1,0,2:T(8,128)(2,1)} copy(bf16[8,128,1,2048]{1,3,2,0:T(8,128)(2,1)} %all-to-all-done) | data formatting | bytes 8388608 | tf_op jit(solution)/shard_map/all_to_all | solution.py:66
  79.1 1.8 %convolution_convert_fusion.5 = bf16[64,2048]{1,0:T(8,128)(2,1)S(1)} fusion(bf16[1024,2048]{1,0:T(8,128)(2,1)} %bitcast.83, s32[]{:T(128)S(6)} %select_n.30, bf16[32,256]{1,0:T(8,128)(2,1)S(1)} %get-tuple-element.22, bf16[32,256]{1,0:T(8,128)(2,1)S(1)} %get-tuple-element.21), kind=kOutput, calls=%fused_computation.10 | convolution fusion | flops 67305472 | bytes 1343492 | tf_op jit(solution)/shard_map/dot_general | solution.py:26
  80.9 1.2 copy.72
  82.1 1.6 convolution_convert_fusion.4
  83.7 1.2 copy.73
  84.9 0.4 convolution_convert_fusion.3
  85.3 1.2 copy.74
  87.0 1.2 copy.75
  88.6 1.2 copy.76
  89.8 0.4 convolution_convert_fusion
  90.2 1.2 copy.77
  91.9 0.7 copy-done.5
  92.6 1.2 copy.71
  93.8 9.9 %stack.100 = bf16[7,2,32,2048]{3,0,2,1:T(8,128)(2,1)S(1)} concatenate(bf16[1,2,32,2048]{3,0,2,1:T(2,128)(2,1)} %copy.71, bf16[1,2,32,2048]{3,0,2,1:T(2,128)(2,1)} %copy.72, bf16[1,2,32,2048]{3,0,2,1:T(2,128)(2,1)} %copy.73, bf16[1,2,32,2048]{3,0,2,1:T(2,128)(2,1)} %copy.74, bf16[1,2,32,2048]{3,0,2,1:T(2,128)(2,1)} %copy.75, bf16[1,2,32,2048]{3,0,2,1:T(2,128)(2,1)} %copy.76, ...), dimensions={0} | concatenate | bytes 3670016 | tf_op jit(solution)/shard_map/stack | solution.py:27
  103.7 1.4 fusion.13
  105.1 1.4 fusion.14
  106.6 1.4 fusion.11
  108.0 0.8 fusion.10
  108.7 1.6 copy.78
  110.4 1.6 copy.79
  112.0 1.6 copy.81
  113.6 0.7 copy.82
  114.3 0.8 add.48
  115.1 0.8 sub.22
  115.9 41.5 %all-reduce = (f32[32,7,7]{0,2,1:T(8,128)}, f32[32,7,7]{0,2,1:T(8,128)S(1)}) all-reduce(f32[32,7,7]{0,2,1:T(8,128)S(1)} %sub.22, f32[32,7,7]{0,2,1:T(8,128)S(1)} %add.48), channel_id=1, replica_groups=mesh['ta'=8,'ga'=4] {'ta','ga'}, use_global_device_ids=true, to_apply=%region_1.2 | all-reduce | flops 3136 | bytes 25088 | tf_op jit(solution)/shard_map/psum | solution.py:73
  157.3 0.6 broadcast_multiply_fusion.1
  158.0 0.9 copy.80
  158.8 2.3 %fusion.12 = f32[32,7,2048]{2,1,0:T(8,128)} fusion(f32[32,7,7]{1,2,0:T(8,128)S(1)} %copy.80, bf16[7,2,32,2048]{3,0,2,1:T(8,128)(2,1)S(1)} %stack.100), kind=kOutput, calls=%fused_computation.24 | convolution fusion | flops 38535168 | bytes 3014656 | tf_op jit(solution)/shard_map/cfp,fcb->bfp/dot_general | solution.py:49
  161.1 1.4 broadcast_multiply_fusion
  162.5 1.5 copy.83
  164.0 2.0 %fusion.9 = f32[32,7,2048]{2,1,0:T(8,128)S(1)} fusion(f32[32,7,7]{1,2,0:T(8,128)} %copy.83, bf16[7,2,32,2048]{3,0,2,1:T(8,128)(2,1)S(1)} %stack.100), kind=kOutput, calls=%fused_computation.21 | convolution fusion | flops 38535168 | bytes 2889856 | tf_op jit(solution)/shard_map/cfp,fcb->bfp/dot_general | solution.py:52
  166.1 2.0 %fusion.1 = f32[7,1,32,2048]{3,0,2,1:T(8,128)S(1)} fusion(f32[32,7,2048]{2,1,0:T(8,128)S(1)} %copy-done.2, f32[32,7,7]{1,2,0:T(8,128)} %copy.83, bf16[7,2,32,2048]{3,0,2,1:T(8,128)(2,1)S(1)} %stack.100), kind=kOutput, calls=%fused_computation.4 | convolution fusion | flops 38993920 | bytes 4987008 | tf_op jit(solution)/shard_map/cfp,fcb->bfp/dot_general | solution.py:49
  168.1 1.1 fusion
  169.2 0.7 maximum_bitcast_fusion
  170.0 4.0 %copy.86 = f32[1,7,2,32,2048]{4,3,2,1,0:T(8,128)} copy(f32[1,7,2,32,2048]{4,1,3,2,0:T(8,128)S(1)} %maximum_bitcast_fusion) | data formatting | bytes 7340032
  174.2 1.2 copy-done.7
  (30 shorter events, 1.7 us)
Async XLA Ops:
  7.0 7.7 %copy-start.1 = (bf16[128,1,16384]{0,2,1:T(8,128)(2,1)S(1)}, bf16[128,1,16384]{0,2,1:T(8,128)(2,1)}, u32[]{:S(2)}) copy-start(bf16[128,1,16384]{0,2,1:T(8,128)(2,1)} %copy.67) | copy-start | bytes 12582916
  18.0 5.3 %copy-start.8 = (s32[7]{0:T(128)S(1)}, s32[7]{0:T(128)}, u32[]{:S(2)}) copy-start(s32[7]{0:T(128)} %param.4) | copy-start | bytes 88
  18.0 18.9 %copy-start.9 = (s32[32]{0:T(128)S(1)}, s32[32]{0:T(128)}, u32[]{:S(2)}) copy-start(s32[32]{0:T(128)} %param.5) | copy-start | bytes 388
  18.0 54.5 %all-to-all-start = ((bf16[8,128,1,2048]{1,3,2,0:T(8,128)(2,1)}), bf16[8,128,1,2048]{1,3,2,0:T(8,128)(2,1)}, u32[]{:S(2)}, u32[]{:S(2)}) async-start(bf16[8,128,1,2048]{1,3,2,0:T(8,128)(2,1)} %fusion.15), calls=%async_computation | async-start | bytes 8388608 | tf_op jit(solution)/shard_map/all_to_all | solution.py:66
  79.1 5.9 %copy-start = (bf16[8,128,1,2048]{3,1,0,2:T(8,128)(2,1)S(1)}, bf16[8,128,1,2048]{3,1,0,2:T(8,128)(2,1)}, u32[]{:S(2)}) copy-start(bf16[8,128,1,2048]{3,1,0,2:T(8,128)(2,1)} %copy.70) | copy-start | bytes 12582916
  90.2 1.6 copy-start.3
  91.9 0.7 copy-start.5
  164.0 2.0 %copy-start.2 = (f32[32,7,2048]{2,1,0:T(8,128)S(1)}, f32[32,7,2048]{2,1,0:T(8,128)}, u32[]{:S(2)}) copy-start(f32[32,7,2048]{2,1,0:T(8,128)} %fusion.12) | copy-start | bytes 5505028
  170.0 4.0 %copy-start.6 = (bf16[64,2048]{1,0:T(8,128)(2,1)S(1)}, bf16[64,2048]{1,0:T(8,128)(2,1)}, u32[]{:S(2)}) copy-start(bf16[64,2048]{1,0:T(8,128)(2,1)} %copy-done.5) | copy-start | bytes 786436
  170.0 4.1 %copy-start.4 = (bf16[64,2048]{1,0:T(8,128)(2,1)S(1)}, bf16[64,2048]{1,0:T(8,128)(2,1)}, u32[]{:S(2)}) copy-start(bf16[64,2048]{1,0:T(8,128)(2,1)} %copy-done.3) | copy-start | bytes 786436
  174.2 1.2 copy-start.7
